TPU v7x, 32 devices: a whole 2x2x4 slice. The times are simulated.
32 devices in a mesh: level: 2 (over core), gx: 4 (over y, x), yz: 4 (over z).
Axes of the slice: x: 2, y: 2, z: 4, core: 2. Of those that a mesh axis runs over, the one named last changes fastest.
Arguments:
- init_field: float32 [128, 64, 256], P('gx', 'yz'), may hold values from -6 to 6
- source: float32 [128, 64, 256], P('gx', 'yz'), may hold values from -4 to 4
- damping: float32 [128, 64, 256], P('gx', 'yz'), may hold values from 0.05 to 2
Outputs:
- final_states: float32 [2, 128, 64, 256], P('level', 'gx', 'yz')
All inputs are finite; a program needn't handle non-finite values.
Results may differ from a plain program's by a relative error of at most 0.0001.
Values sent between devices are 32-bit elements; how exact they have to be, the bound alone decides.
A program may use at most 64 MiB of HBM per device.

v0:
```python
import jax
import jax.numpy as jnp
from jax import lax
from jax.sharding import PartitionSpec as P

STEPS = 3
ITERS = 3
diffusion_number = 1.0


def extended(cells, sides, width):
    for axis, dim in sides:
        count = lax.axis_size(axis)
        ends = count - 1
        head = lax.slice_in_dim(cells, 0, width, axis=dim)
        tail = lax.slice_in_dim(cells, cells.shape[dim] - width, cells.shape[dim], axis=dim)
        cells = jnp.concatenate(
            [
                lax.ppermute(tail, axis, [(i, (i + 1) % count) for i in range(ends)]),
                cells,
                lax.ppermute(head, axis, [((i + 1) % count, i) for i in range(ends)]),
            ],
            axis=dim,
        )
    return cells


def passed_along(block, axis, distance):
    devices = range(lax.axis_size(axis))
    route = [(i - distance, i) for i in devices if i - distance in devices]
    return lax.ppermute(block, axis, route)


def stencil_from(padded, field, damping):
    beside = padded[2:, 1:-1, :] + padded[:-2, 1:-1, :]
    beside = beside + padded[1:-1, 2:, :] + padded[1:-1, :-2, :]
    zero_plane = jnp.zeros_like(field[:, :, :1])
    beside = beside + jnp.concatenate([field[:, :, 1:], zero_plane], axis=2)
    beside = beside + jnp.concatenate([zero_plane, field[:, :, :-1]], axis=2)
    return damping * field + diffusion_number * (6.0 * field - beside)


def operate(field, damping):
    padded = extended(field, (("gx", 0), ("yz", 1)), 1)
    return field + stencil_from(padded, field, damping)


def two_products(resid, image):
    return lax.psum((jnp.sum(resid * resid), jnp.sum(resid * image)), ("gx", "yz"))


def solve(target, guess, damping):
    answer = guess
    resid = target - operate(answer, damping)
    image = operate(resid, damping)
    norm_now, product = two_products(resid, image)
    alpha = norm_now / product
    direction, along = (resid, image)
    for step in range(ITERS):
        answer = answer + alpha * direction
        resid = resid - alpha * along
        if step + 1 < ITERS:
            image = operate(resid, damping)
            norm_next, product = two_products(resid, image)
            ratio = norm_next / norm_now
            alpha = norm_next / (product - ratio * norm_next / alpha)
            direction = resid + ratio * direction
            along = image + ratio * along
            norm_now = norm_next
    return answer


def per_device(init_field, source, damping):
    upper = lax.axis_index("level") == 1
    state = init_field
    older = jnp.where(upper, init_field, jnp.zeros_like(init_field))
    for rounds in range(STEPS + 1):
        if rounds == 0:
            extra = jnp.zeros_like(init_field)
        else:
            incoming = passed_along(state, "level", 1)
            change = incoming - older
            older = incoming
            padded = extended(change, (("gx", 0), ("yz", 1)), 1)
            extra = 0.5 * stencil_from(padded, change, damping)
        fresh = solve(state + source + extra, state, damping)
        if rounds == 0:
            state = jnp.where(upper, state, fresh)
        elif rounds == STEPS:
            state = jnp.where(upper, fresh, state)
        else:
            state = fresh
    return state[None]


def solution(mesh):
    in_specs = (P("gx", "yz", None), P("gx", "yz", None), P("gx", "yz", None))
    out_specs = P("level", "gx", "yz", None)
    return jax.shard_map(
        per_device, mesh=mesh, in_specs=in_specs, out_specs=out_specs, check_vma=False
    )
```

profile of v0, /device:TPU:0, one launch (start us, length us, event | category | flops | bytes accessed | tf_op | source)
XLA Modules:
  0.0 858.0 jit_solution(10552199963659555347)
XLA Ops:
  0.7 4.9 collective-permute-start.1
  38.3 40.1 %all-reduce.49 = (f32[]{:T(128)}, f32[]{:T(128)}) all-reduce(f32[]{:T(128)} %get-tuple-element.28, f32[]{:T(128)} %get-tuple-element.27), channel_id=1, replica_groups=mesh['level'=2,'gx'=4,'yz'=4] {'gx','yz'}, use_global_device_ids=true, to_apply=%region_1.2 | all-reduce | flops 2 | bytes 16 | tf_op jit(solution)/shard_map/psum | solution.py:49
  83.3 8.2 collective-permute-done.8
  100.9 39.7 %all-reduce.48 = (f32[]{:T(128)}, f32[]{:T(128)}) all-reduce(f32[]{:T(128)} %get-tuple-element.26, f32[]{:T(128)} %get-tuple-element.25), channel_id=1, replica_groups=mesh['level'=2,'gx'=4,'yz'=4] {'gx','yz'}, use_global_device_ids=true, to_apply=%region_5.6 | all-reduce | flops 2 | bytes 16 | tf_op jit(solution)/shard_map/psum | solution.py:49
  149.0 5.5 collective-permute-done.12
  163.2 39.7 %all-reduce.47 = (f32[]{:T(128)}, f32[]{:T(128)}) all-reduce(f32[]{:T(128)} %get-tuple-element.24, f32[]{:T(128)} %get-tuple-element.23), channel_id=1, replica_groups=mesh['level'=2,'gx'=4,'yz'=4] {'gx','yz'}, use_global_device_ids=true, to_apply=%region_9.10 | all-reduce | flops 2 | bytes 16 | tf_op jit(solution)/shard_map/psum | solution.py:49
  212.1 7.1 collective-permute-start.18
  234.9 5.4 collective-permute-start.26
  241.8 5.1 collective-permute-done.25
  255.8 39.8 %all-reduce.46 = (f32[]{:T(128)}, f32[]{:T(128)}) all-reduce(f32[]{:T(128)} %get-tuple-element.22, f32[]{:T(128)} %get-tuple-element.21), channel_id=1, replica_groups=mesh['level'=2,'gx'=4,'yz'=4] {'gx','yz'}, use_global_device_ids=true, to_apply=%region_13.14 | all-reduce | flops 2 | bytes 16 | tf_op jit(solution)/shard_map/psum | solution.py:49
  299.6 8.9 %collective-permute-done.29 = f32[1,16,256]{2,1,0:T(8,128)S(1)} collective-permute-done((f32[1,16,256]{2,1,0:T(8,128)S(1)}, f32[1,16,256]{2,1,0:T(8,128)S(1)}, u32[]{:S(2)}, u32[]{:S(2)}) %collective-permute-start.29) | collective-permute-done | bytes 16416 | tf_op jit(solution)/shard_map/ppermute | solution.py:21
  317.9 39.7 %all-reduce.45 = (f32[]{:T(128)}, f32[]{:T(128)}) all-reduce(f32[]{:T(128)} %get-tuple-element.20, f32[]{:T(128)} %get-tuple-element.19), channel_id=1, replica_groups=mesh['level'=2,'gx'=4,'yz'=4] {'gx','yz'}, use_global_device_ids=true, to_apply=%region_17.18 | all-reduce | flops 2 | bytes 16 | tf_op jit(solution)/shard_map/psum | solution.py:49
  366.0 5.5 collective-permute-done.33
  380.0 39.7 %all-reduce.44 = (f32[]{:T(128)}, f32[]{:T(128)}) all-reduce(f32[]{:T(128)} %get-tuple-element.18, f32[]{:T(128)} %get-tuple-element.17), channel_id=1, replica_groups=mesh['level'=2,'gx'=4,'yz'=4] {'gx','yz'}, use_global_device_ids=true, to_apply=%region_21.22 | all-reduce | flops 2 | bytes 16 | tf_op jit(solution)/shard_map/psum | solution.py:49
  428.8 7.2 collective-permute-start.39
  444.6 4.9 collective-permute-start.41
  451.7 5.4 collective-permute-start.47
  458.5 5.1 collective-permute-done.46
  465.0 4.9 collective-permute-start.49
  472.6 39.8 %all-reduce.43 = (f32[]{:T(128)}, f32[]{:T(128)}) all-reduce(f32[]{:T(128)} %get-tuple-element.16, f32[]{:T(128)} %get-tuple-element.15), channel_id=1, replica_groups=mesh['level'=2,'gx'=4,'yz'=4] {'gx','yz'}, use_global_device_ids=true, to_apply=%region_25.26 | all-reduce | flops 2 | bytes 16 | tf_op jit(solution)/shard_map/psum | solution.py:49
  516.4 8.9 %collective-permute-done.50 = f32[1,16,256]{2,1,0:T(8,128)S(1)} collective-permute-done((f32[1,16,256]{2,1,0:T(8,128)S(1)}, f32[1,16,256]{2,1,0:T(8,128)S(1)}, u32[]{:S(2)}, u32[]{:S(2)}) %collective-permute-start.50) | collective-permute-done | bytes 16416 | tf_op jit(solution)/shard_map/ppermute | solution.py:21
  534.7 39.8 %all-reduce.42 = (f32[]{:T(128)}, f32[]{:T(128)}) all-reduce(f32[]{:T(128)} %get-tuple-element.14, f32[]{:T(128)} %get-tuple-element.13), channel_id=1, replica_groups=mesh['level'=2,'gx'=4,'yz'=4] {'gx','yz'}, use_global_device_ids=true, to_apply=%region_29.30 | all-reduce | flops 2 | bytes 16 | tf_op jit(solution)/shard_map/psum | solution.py:49
  582.8 5.4 collective-permute-done.54
  596.9 39.7 %all-reduce.41 = (f32[]{:T(128)}, f32[]{:T(128)}) all-reduce(f32[]{:T(128)} %get-tuple-element.12, f32[]{:T(128)} %get-tuple-element.11), channel_id=1, replica_groups=mesh['level'=2,'gx'=4,'yz'=4] {'gx','yz'}, use_global_device_ids=true, to_apply=%region_33.34 | all-reduce | flops 2 | bytes 16 | tf_op jit(solution)/shard_map/psum | solution.py:49
  644.9 7.2 collective-permute-start.60
  667.8 5.4 collective-permute-start.68
  674.7 5.1 collective-permute-done.67
  688.6 39.8 %all-reduce.40 = (f32[]{:T(128)}, f32[]{:T(128)}) all-reduce(f32[]{:T(128)} %get-tuple-element.10, f32[]{:T(128)} %get-tuple-element.9), channel_id=1, replica_groups=mesh['level'=2,'gx'=4,'yz'=4] {'gx','yz'}, use_global_device_ids=true, to_apply=%region_37.38 | all-reduce | flops 2 | bytes 16 | tf_op jit(solution)/shard_map/psum | solution.py:49
  732.7 8.9 %collective-permute-done.71 = f32[1,16,256]{2,1,0:T(8,128)S(1)} collective-permute-done((f32[1,16,256]{2,1,0:T(8,128)S(1)}, f32[1,16,256]{2,1,0:T(8,128)S(1)}, u32[]{:S(2)}, u32[]{:S(2)}) %collective-permute-start.71) | collective-permute-done | bytes 16416 | tf_op jit(solution)/shard_map/ppermute | solution.py:21
  751.0 39.7 %all-reduce.39 = (f32[]{:T(128)}, f32[]{:T(128)}) all-reduce(f32[]{:T(128)} %get-tuple-element.8, f32[]{:T(128)} %get-tuple-element.7), channel_id=1, replica_groups=mesh['level'=2,'gx'=4,'yz'=4] {'gx','yz'}, use_global_device_ids=true, to_apply=%region_41.42 | all-reduce | flops 2 | bytes 16 | tf_op jit(solution)/shard_map/psum | solution.py:49
  799.2 5.5 collective-permute-done.75
  813.3 39.7 %all-reduce.38 = (f32[]{:T(128)}, f32[]{:T(128)}) all-reduce(f32[]{:T(128)} %get-tuple-element.6, f32[]{:T(128)} %get-tuple-element.5), channel_id=1, replica_groups=mesh['level'=2,'gx'=4,'yz'=4] {'gx','yz'}, use_global_device_ids=true, to_apply=%region_45.46 | all-reduce | flops 2 | bytes 16 | tf_op jit(solution)/shard_map/psum | solution.py:49
  (249 shorter events, 216.7 us)
Async XLA Ops:
  81.9 9.6 %collective-permute-start.8 = (f32[1,16,256]{2,1,0:T(8,128)S(1)}, f32[1,16,256]{2,1,0:T(8,128)S(1)}, u32[]{:S(2)}, u32[]{:S(2)}) collective-permute-start(f32[1,16,256]{2,1,0:T(8,128)S(1)} %get-tuple-element.164), channel_id=1, source_target_pairs={{4,0},{8,4},{12,8},{5,1},{9,5},{13,9},{6,2},{10,6},{14,10},{7,3},{... | collective-permute-start | bytes 49160 | tf_op jit(solution)/shard_map/ppermute | solution.py:21
  147.6 7.0 collective-permute-start.12
  208.4 12.0 %collective-permute-start.22 = (f32[1,16,256]{2,1,0:T(8,128)S(1)}, f32[1,16,256]{2,1,0:T(8,128)S(1)}, u32[]{:S(2)}, u32[]{:S(2)}) collective-permute-start(f32[1,16,256]{2,1,0:T(8,128)S(1)} %get-tuple-element.157), channel_id=1, source_target_pairs={{0,4},{4,8},{8,12},{1,5},{5,9},{9,13},{2,6},{6,10},{10,14},{3,7},{... | collective-permute-start | bytes 49160 | tf_op jit(solution)/shard_map/ppermute | solution.py:19
  209.7 10.7 %collective-permute-start.21 = (f32[1,16,256]{2,1,0:T(8,128)S(1)}, f32[1,16,256]{2,1,0:T(8,128)S(1)}, u32[]{:S(2)}, u32[]{:S(2)}) collective-permute-start(f32[1,16,256]{2,1,0:T(8,128)S(1)} %get-tuple-element.158), channel_id=1, source_target_pairs={{4,0},{8,4},{12,8},{5,1},{9,5},{13,9},{6,2},{10,6},{14,10},{7,3},{... | collective-permute-start | bytes 49160 | tf_op jit(solution)/shard_map/ppermute | solution.py:21
  212.1 14.3 %collective-permute-start.18 = (f32[1,16,256]{2,1,0:T(8,128)S(1)}, f32[1,16,256]{2,1,0:T(8,128)S(1)}, u32[]{:S(2)}, u32[]{:S(2)}) collective-permute-start(f32[1,16,256]{2,1,0:T(8,128)S(1)} %get-tuple-element.155), channel_id=1, source_target_pairs={{0,4},{4,8},{8,12},{1,5},{5,9},{9,13},{2,6},{6,10},{10,14},{3,7},{... | collective-permute-start | bytes 49160 | tf_op jit(solution)/shard_map/ppermute | solution.py:19
  219.2 7.2 collective-permute-start.17
  220.5 12.2 %collective-permute-start.23 = (f32[34,1,256]{2,1,0:T(1,128)S(1)}, f32[34,1,256]{2,1,0:T(1,128)S(1)}, u32[]{:S(2)}, u32[]{:S(2)}) collective-permute-start(f32[34,1,256]{2,1,0:T(1,128)S(1)} %get-tuple-element.89), channel_id=1, source_target_pairs={{1,0},{2,1},{3,2},{5,4},{6,5},{7,6},{9,8},{10,9},{11,10},{13,12},{... | collective-permute-start | bytes 104456 | tf_op jit(solution)/shard_map/ppermute | solution.py:21
  221.8 10.9 %collective-permute-start.24 = (f32[34,1,256]{2,1,0:T(1,128)S(1)}, f32[34,1,256]{2,1,0:T(1,128)S(1)}, u32[]{:S(2)}, u32[]{:S(2)}) collective-permute-start(f32[34,1,256]{2,1,0:T(1,128)S(1)} %get-tuple-element.90), channel_id=1, source_target_pairs={{0,1},{1,2},{2,3},{4,5},{5,6},{6,7},{8,9},{9,10},{10,11},{12,13},{... | collective-permute-start | bytes 104456 | tf_op jit(solution)/shard_map/ppermute | solution.py:19
  234.9 6.9 collective-permute-start.26
  240.3 6.5 collective-permute-start.25
  298.2 10.3 %collective-permute-start.29 = (f32[1,16,256]{2,1,0:T(8,128)S(1)}, f32[1,16,256]{2,1,0:T(8,128)S(1)}, u32[]{:S(2)}, u32[]{:S(2)}) collective-permute-start(f32[1,16,256]{2,1,0:T(8,128)S(1)} %get-tuple-element.144), channel_id=1, source_target_pairs={{4,0},{8,4},{12,8},{5,1},{9,5},{13,9},{6,2},{10,6},{14,10},{7,3},{... | collective-permute-start | bytes 49160 | tf_op jit(solution)/shard_map/ppermute | solution.py:21
  364.5 6.9 collective-permute-start.33
  425.0 12.3 %collective-permute-start.43 = (f32[1,16,256]{2,1,0:T(8,128)S(1)}, f32[1,16,256]{2,1,0:T(8,128)S(1)}, u32[]{:S(2)}, u32[]{:S(2)}) collective-permute-start(f32[1,16,256]{2,1,0:T(8,128)S(1)} %get-tuple-element.137), channel_id=1, source_target_pairs={{0,4},{4,8},{8,12},{1,5},{5,9},{9,13},{2,6},{6,10},{10,14},{3,7},{... | collective-permute-start | bytes 49160 | tf_op jit(solution)/shard_map/ppermute | solution.py:19
  426.3 11.0 %collective-permute-start.42 = (f32[1,16,256]{2,1,0:T(8,128)S(1)}, f32[1,16,256]{2,1,0:T(8,128)S(1)}, u32[]{:S(2)}, u32[]{:S(2)}) collective-permute-start(f32[1,16,256]{2,1,0:T(8,128)S(1)} %get-tuple-element.138), channel_id=1, source_target_pairs={{4,0},{8,4},{12,8},{5,1},{9,5},{13,9},{6,2},{10,6},{14,10},{7,3},{... | collective-permute-start | bytes 49160 | tf_op jit(solution)/shard_map/ppermute | solution.py:21
  428.8 14.4 %collective-permute-start.39 = (f32[1,16,256]{2,1,0:T(8,128)S(1)}, f32[1,16,256]{2,1,0:T(8,128)S(1)}, u32[]{:S(2)}, u32[]{:S(2)}) collective-permute-start(f32[1,16,256]{2,1,0:T(8,128)S(1)} %get-tuple-element.135), channel_id=1, source_target_pairs={{0,4},{4,8},{8,12},{1,5},{5,9},{9,13},{2,6},{6,10},{10,14},{3,7},{... | collective-permute-start | bytes 49160 | tf_op jit(solution)/shard_map/ppermute | solution.py:19
  435.9 7.2 collective-permute-start.38
  437.3 12.3 %collective-permute-start.44 = (f32[34,1,256]{2,1,0:T(1,128)S(1)}, f32[34,1,256]{2,1,0:T(1,128)S(1)}, u32[]{:S(2)}, u32[]{:S(2)}) collective-permute-start(f32[34,1,256]{2,1,0:T(1,128)S(1)} %get-tuple-element.79), channel_id=1, source_target_pairs={{1,0},{2,1},{3,2},{5,4},{6,5},{7,6},{9,8},{10,9},{11,10},{13,12},{... | collective-permute-start | bytes 104456 | tf_op jit(solution)/shard_map/ppermute | solution.py:21
  438.6 11.0 %collective-permute-start.45 = (f32[34,1,256]{2,1,0:T(1,128)S(1)}, f32[34,1,256]{2,1,0:T(1,128)S(1)}, u32[]{:S(2)}, u32[]{:S(2)}) collective-permute-start(f32[34,1,256]{2,1,0:T(1,128)S(1)} %get-tuple-element.80), channel_id=1, source_target_pairs={{0,1},{1,2},{2,3},{4,5},{5,6},{6,7},{8,9},{9,10},{10,11},{12,13},{... | collective-permute-start | bytes 104456 | tf_op jit(solution)/shard_map/ppermute | solution.py:19
  451.7 6.9 collective-permute-start.47
  457.1 6.5 collective-permute-start.46
  515.0 10.4 %collective-permute-start.50 = (f32[1,16,256]{2,1,0:T(8,128)S(1)}, f32[1,16,256]{2,1,0:T(8,128)S(1)}, u32[]{:S(2)}, u32[]{:S(2)}) collective-permute-start(f32[1,16,256]{2,1,0:T(8,128)S(1)} %get-tuple-element.124), channel_id=1, source_target_pairs={{4,0},{8,4},{12,8},{5,1},{9,5},{13,9},{6,2},{10,6},{14,10},{7,3},{... | collective-permute-start | bytes 49160 | tf_op jit(solution)/shard_map/ppermute | solution.py:21
  581.4 6.9 collective-permute-start.54
  641.8 11.6 %collective-permute-start.64 = (f32[1,16,256]{2,1,0:T(8,128)S(1)}, f32[1,16,256]{2,1,0:T(8,128)S(1)}, u32[]{:S(2)}, u32[]{:S(2)}) collective-permute-start(f32[1,16,256]{2,1,0:T(8,128)S(1)} %get-tuple-element.117), channel_id=1, source_target_pairs={{0,4},{4,8},{8,12},{1,5},{5,9},{9,13},{2,6},{6,10},{10,14},{3,7},{... | collective-permute-start | bytes 49160 | tf_op jit(solution)/shard_map/ppermute | solution.py:19
  643.1 10.3 %collective-permute-start.63 = (f32[1,16,256]{2,1,0:T(8,128)S(1)}, f32[1,16,256]{2,1,0:T(8,128)S(1)}, u32[]{:S(2)}, u32[]{:S(2)}) collective-permute-start(f32[1,16,256]{2,1,0:T(8,128)S(1)} %get-tuple-element.118), channel_id=1, source_target_pairs={{4,0},{8,4},{12,8},{5,1},{9,5},{13,9},{6,2},{10,6},{14,10},{7,3},{... | collective-permute-start | bytes 49160 | tf_op jit(solution)/shard_map/ppermute | solution.py:21
  644.9 14.4 %collective-permute-start.60 = (f32[1,16,256]{2,1,0:T(8,128)S(1)}, f32[1,16,256]{2,1,0:T(8,128)S(1)}, u32[]{:S(2)}, u32[]{:S(2)}) collective-permute-start(f32[1,16,256]{2,1,0:T(8,128)S(1)} %get-tuple-element.115), channel_id=1, source_target_pairs={{0,4},{4,8},{8,12},{1,5},{5,9},{9,13},{2,6},{6,10},{10,14},{3,7},{... | collective-permute-start | bytes 49160 | tf_op jit(solution)/shard_map/ppermute | solution.py:19
  652.1 7.2 collective-permute-start.59
  653.4 12.2 %collective-permute-start.65 = (f32[34,1,256]{2,1,0:T(1,128)S(1)}, f32[34,1,256]{2,1,0:T(1,128)S(1)}, u32[]{:S(2)}, u32[]{:S(2)}) collective-permute-start(f32[34,1,256]{2,1,0:T(1,128)S(1)} %get-tuple-element.69), channel_id=1, source_target_pairs={{1,0},{2,1},{3,2},{5,4},{6,5},{7,6},{9,8},{10,9},{11,10},{13,12},{... | collective-permute-start | bytes 104456 | tf_op jit(solution)/shard_map/ppermute | solution.py:21
  654.7 10.9 %collective-permute-start.66 = (f32[34,1,256]{2,1,0:T(1,128)S(1)}, f32[34,1,256]{2,1,0:T(1,128)S(1)}, u32[]{:S(2)}, u32[]{:S(2)}) collective-permute-start(f32[34,1,256]{2,1,0:T(1,128)S(1)} %get-tuple-element.70), channel_id=1, source_target_pairs={{0,1},{1,2},{2,3},{4,5},{5,6},{6,7},{8,9},{9,10},{10,11},{12,13},{... | collective-permute-start | bytes 104456 | tf_op jit(solution)/shard_map/ppermute | solution.py:19
  667.8 6.9 collective-permute-start.68
  673.2 6.5 collective-permute-start.67
  731.3 10.4 %collective-permute-start.71 = (f32[1,16,256]{2,1,0:T(8,128)S(1)}, f32[1,16,256]{2,1,0:T(8,128)S(1)}, u32[]{:S(2)}, u32[]{:S(2)}) collective-permute-start(f32[1,16,256]{2,1,0:T(8,128)S(1)} %get-tuple-element.104), channel_id=1, source_target_pairs={{4,0},{8,4},{12,8},{5,1},{9,5},{13,9},{6,2},{10,6},{14,10},{7,3},{... | collective-permute-start | bytes 49160 | tf_op jit(solution)/shard_map/ppermute | solution.py:21
  797.7 6.9 collective-permute-start.75
  (57 other events, 304.7 us)
where the time goes:
time: 861 us; the launch traced here: 858 us
  blocking collectives  477 us (55%)
  starting transfers between devices  204 us (24%)
  waiting for transfers between devices  103 us (12%)
  between operations  39.6 us (5%)
  other arithmetic  27.4 us (3%)
    psum x12, blocking collectives, two_products(): lax.psum((jnp.sum(resid * resid), jnp.sum(resid * image)), ('gx', 'yz'))  477 us
    ppermute x38, starting transfers between devices, extended(): lax.ppermute(tail, axis, [(i, (i + 1) % count) for i in range(ends)])  150 us
    ppermute x38, waiting for transfers between devices, extended(): lax.ppermute(head, axis, [((i + 1) % count, i) for i in range(ends)])  79.6 us
    ppermute x38, starting transfers between devices, extended(): lax.ppermute(head, axis, [((i + 1) % count, i) for i in range(ends)])  49.4 us
    ppermute x38, waiting for transfers between devices, extended(): lax.ppermute(tail, axis, [(i, (i + 1) % count) for i in range(ends)])  23.4 us
  transfers between devices with their start and end apart: 79, of which 42 were waited for; matrix products, arithmetic and copies ran while one was open for 1% of the time, Pallas kernels for 0%

commit v1 on v0

--- a/solution.py
+++ b/solution.py
@@ -46,7 +46,7 @@
 
 
 def two_products(resid, image):
-    return lax.psum((jnp.sum(resid * resid), jnp.sum(resid * image)), ("gx", "yz"))
+    return lax.psum(lax.psum((jnp.sum(resid * resid), jnp.sum(resid * image)), "yz"), "gx")
 
 
 def solve(target, guess, damping):

time: 861 us -> 641 us (0.74)
  blocking collectives: 477 us -> 272 us
  waiting for transfers between devices: 103 us -> 88.5 us
    psum x12 -> x24, blocking collectives: 477 us -> 272 us  [the longest x12 141 us: two_products(): lax.psum((jnp.sum(resid * resid), jnp.sum(resid * image)), 'yz')]
    ppermute x38, waiting for transfers between devices: 79.6 us -> 64.9 us  [extended(): lax.ppermute(head, axis, [((i + 1) % count, i) for i in range(ends)])]
where the time goes in v1:
time: 641 us; the launch traced here: 637 us
  blocking collectives  272 us (42%)
  starting transfers between devices  203 us (32%)
  waiting for transfers between devices  88.5 us (14%)
  between operations  39.3 us (6%)
  other arithmetic  27.1 us (4%)
  local copies, waits for them, and re-layouts  7.39 us (1%)
    ppermute x38, starting transfers between devices, extended(): lax.ppermute(tail, axis, [(i, (i + 1) % count) for i in range(ends)])  150 us
    psum x12, blocking collectives, two_products(): lax.psum((jnp.sum(resid * resid), jnp.sum(resid * image)), 'yz')  141 us
    psum x12, blocking collectives, two_products(): lax.psum(lax.psum((jnp.sum(resid * resid), jnp.sum(resid * image)), 'yz')...  131 us
    ppermute x38, waiting for transfers between devices, extended(): lax.ppermute(head, axis, [((i + 1) % count, i) for i in range(ends)])  64.9 us
    ppermute x38, starting transfers between devices, extended(): lax.ppermute(head, axis, [((i + 1) % count, i) for i in range(ends)])  49.5 us
    ppermute x38, waiting for transfers between devices, extended(): lax.ppermute(tail, axis, [(i, (i + 1) % count) for i in range(ends)])  23.6 us
    reduce_sum x12, other arithmetic, two_products(): jnp.sum(resid * image)  16 us
  transfers between devices with their start and end apart: 79, of which 42 were waited for; matrix products, arithmetic and copies ran while one was open for 1% of the time, Pallas kernels for 0%

profile of v1, /device:TPU:0, one launch (start us, length us, event | category | flops | bytes accessed | tf_op | source)
XLA Modules:
  0.0 637.2 jit_solution(3748234381024883464)
XLA Ops:
  38.2 13.8 %all-reduce.49 = (f32[]{:T(128)}, f32[]{:T(128)}) all-reduce(f32[]{:T(128)} %get-tuple-element.28, f32[]{:T(128)} %get-tuple-element.27), channel_id=1, replica_groups=mesh['level'=2,'gx'=4,'yz'=4] {'yz'}, use_global_device_ids=true, to_apply=%region_1.2 | all-reduce | flops 2 | bytes 16 | tf_op jit(solution)/shard_map/psum | solution.py:49
  52.0 9.6 %all-reduce.61 = (f32[]{:T(128)}, f32[]{:T(128)}) all-reduce(f32[]{:T(128)} %get-tuple-element.51, f32[]{:T(128)} %get-tuple-element.52), channel_id=1, replica_groups=mesh['level'=2,'gx'=4,'yz'=4] {'gx'}, use_global_device_ids=true, to_apply=%region_2.3 | all-reduce | flops 2 | bytes 16 | tf_op jit(solution)/shard_map/psum | solution.py:49
  80.8 11.3 %all-reduce.48 = (f32[]{:T(128)}, f32[]{:T(128)}) all-reduce(f32[]{:T(128)} %get-tuple-element.26, f32[]{:T(128)} %get-tuple-element.25), channel_id=1, replica_groups=mesh['level'=2,'gx'=4,'yz'=4] {'yz'}, use_global_device_ids=true, to_apply=%region_7.8 | all-reduce | flops 2 | bytes 16 | tf_op jit(solution)/shard_map/psum | solution.py:49
  92.1 11.0 %all-reduce.60 = (f32[]{:T(128)}, f32[]{:T(128)}) all-reduce(f32[]{:T(128)} %get-tuple-element.49, f32[]{:T(128)} %get-tuple-element.50), channel_id=1, replica_groups=mesh['level'=2,'gx'=4,'yz'=4] {'gx'}, use_global_device_ids=true, to_apply=%region_8.9 | all-reduce | flops 2 | bytes 16 | tf_op jit(solution)/shard_map/psum | solution.py:49
  111.8 5.4 collective-permute-done.12
  125.8 11.3 %all-reduce.47 = (f32[]{:T(128)}, f32[]{:T(128)}) all-reduce(f32[]{:T(128)} %get-tuple-element.24, f32[]{:T(128)} %get-tuple-element.23), channel_id=1, replica_groups=mesh['level'=2,'gx'=4,'yz'=4] {'yz'}, use_global_device_ids=true, to_apply=%region_13.14 | all-reduce | flops 2 | bytes 16 | tf_op jit(solution)/shard_map/psum | solution.py:49
  137.0 11.0 %all-reduce.59 = (f32[]{:T(128)}, f32[]{:T(128)}) all-reduce(f32[]{:T(128)} %get-tuple-element.47, f32[]{:T(128)} %get-tuple-element.48), channel_id=1, replica_groups=mesh['level'=2,'gx'=4,'yz'=4] {'gx'}, use_global_device_ids=true, to_apply=%region_14.15 | all-reduce | flops 2 | bytes 16 | tf_op jit(solution)/shard_map/psum | solution.py:49
  157.5 5.7 collective-permute-start.18
  178.9 5.4 collective-permute-start.26
  199.8 12.2 %all-reduce.46 = (f32[]{:T(128)}, f32[]{:T(128)}) all-reduce(f32[]{:T(128)} %get-tuple-element.22, f32[]{:T(128)} %get-tuple-element.21), channel_id=1, replica_groups=mesh['level'=2,'gx'=4,'yz'=4] {'yz'}, use_global_device_ids=true, to_apply=%region_19.20 | all-reduce | flops 2 | bytes 16 | tf_op jit(solution)/shard_map/psum | solution.py:49
  212.0 11.0 %all-reduce.58 = (f32[]{:T(128)}, f32[]{:T(128)}) all-reduce(f32[]{:T(128)} %get-tuple-element.45, f32[]{:T(128)} %get-tuple-element.46), channel_id=1, replica_groups=mesh['level'=2,'gx'=4,'yz'=4] {'gx'}, use_global_device_ids=true, to_apply=%region_20.21 | all-reduce | flops 2 | bytes 16 | tf_op jit(solution)/shard_map/psum | solution.py:49
  227.5 5.4 collective-permute-done.29
  242.3 11.3 %all-reduce.45 = (f32[]{:T(128)}, f32[]{:T(128)}) all-reduce(f32[]{:T(128)} %get-tuple-element.20, f32[]{:T(128)} %get-tuple-element.19), channel_id=1, replica_groups=mesh['level'=2,'gx'=4,'yz'=4] {'yz'}, use_global_device_ids=true, to_apply=%region_25.26 | all-reduce | flops 2 | bytes 16 | tf_op jit(solution)/shard_map/psum | solution.py:49
  253.6 11.0 %all-reduce.57 = (f32[]{:T(128)}, f32[]{:T(128)}) all-reduce(f32[]{:T(128)} %get-tuple-element.43, f32[]{:T(128)} %get-tuple-element.44), channel_id=1, replica_groups=mesh['level'=2,'gx'=4,'yz'=4] {'gx'}, use_global_device_ids=true, to_apply=%region_26.27 | all-reduce | flops 2 | bytes 16 | tf_op jit(solution)/shard_map/psum | solution.py:49
  287.3 11.3 %all-reduce.44 = (f32[]{:T(128)}, f32[]{:T(128)}) all-reduce(f32[]{:T(128)} %get-tuple-element.18, f32[]{:T(128)} %get-tuple-element.17), channel_id=1, replica_groups=mesh['level'=2,'gx'=4,'yz'=4] {'yz'}, use_global_device_ids=true, to_apply=%region_31.32 | all-reduce | flops 2 | bytes 16 | tf_op jit(solution)/shard_map/psum | solution.py:49
  298.6 11.0 %all-reduce.56 = (f32[]{:T(128)}, f32[]{:T(128)}) all-reduce(f32[]{:T(128)} %get-tuple-element.41, f32[]{:T(128)} %get-tuple-element.42), channel_id=1, replica_groups=mesh['level'=2,'gx'=4,'yz'=4] {'gx'}, use_global_device_ids=true, to_apply=%region_32.33 | all-reduce | flops 2 | bytes 16 | tf_op jit(solution)/shard_map/psum | solution.py:49
  319.2 5.7 collective-permute-start.39
  340.8 5.4 collective-permute-start.47
  361.7 12.2 %all-reduce.43 = (f32[]{:T(128)}, f32[]{:T(128)}) all-reduce(f32[]{:T(128)} %get-tuple-element.16, f32[]{:T(128)} %get-tuple-element.15), channel_id=1, replica_groups=mesh['level'=2,'gx'=4,'yz'=4] {'yz'}, use_global_device_ids=true, to_apply=%region_37.38 | all-reduce | flops 2 | bytes 16 | tf_op jit(solution)/shard_map/psum | solution.py:49
  373.9 11.0 %all-reduce.55 = (f32[]{:T(128)}, f32[]{:T(128)}) all-reduce(f32[]{:T(128)} %get-tuple-element.39, f32[]{:T(128)} %get-tuple-element.40), channel_id=1, replica_groups=mesh['level'=2,'gx'=4,'yz'=4] {'gx'}, use_global_device_ids=true, to_apply=%region_38.39 | all-reduce | flops 2 | bytes 16 | tf_op jit(solution)/shard_map/psum | solution.py:49
  404.2 11.3 %all-reduce.42 = (f32[]{:T(128)}, f32[]{:T(128)}) all-reduce(f32[]{:T(128)} %get-tuple-element.14, f32[]{:T(128)} %get-tuple-element.13), channel_id=1, replica_groups=mesh['level'=2,'gx'=4,'yz'=4] {'yz'}, use_global_device_ids=true, to_apply=%region_43.44 | all-reduce | flops 2 | bytes 16 | tf_op jit(solution)/shard_map/psum | solution.py:49
  415.5 11.0 %all-reduce.54 = (f32[]{:T(128)}, f32[]{:T(128)}) all-reduce(f32[]{:T(128)} %get-tuple-element.37, f32[]{:T(128)} %get-tuple-element.38), channel_id=1, replica_groups=mesh['level'=2,'gx'=4,'yz'=4] {'gx'}, use_global_device_ids=true, to_apply=%region_44.45 | all-reduce | flops 2 | bytes 16 | tf_op jit(solution)/shard_map/psum | solution.py:49
  449.2 11.3 %all-reduce.41 = (f32[]{:T(128)}, f32[]{:T(128)}) all-reduce(f32[]{:T(128)} %get-tuple-element.12, f32[]{:T(128)} %get-tuple-element.11), channel_id=1, replica_groups=mesh['level'=2,'gx'=4,'yz'=4] {'yz'}, use_global_device_ids=true, to_apply=%region_49.50 | all-reduce | flops 2 | bytes 16 | tf_op jit(solution)/shard_map/psum | solution.py:49
  460.5 11.0 %all-reduce.53 = (f32[]{:T(128)}, f32[]{:T(128)}) all-reduce(f32[]{:T(128)} %get-tuple-element.35, f32[]{:T(128)} %get-tuple-element.36), channel_id=1, replica_groups=mesh['level'=2,'gx'=4,'yz'=4] {'gx'}, use_global_device_ids=true, to_apply=%region_50.51 | all-reduce | flops 2 | bytes 16 | tf_op jit(solution)/shard_map/psum | solution.py:49
  480.4 5.7 collective-permute-start.60
  501.8 5.4 collective-permute-start.68
  522.7 12.2 %all-reduce.40 = (f32[]{:T(128)}, f32[]{:T(128)}) all-reduce(f32[]{:T(128)} %get-tuple-element.10, f32[]{:T(128)} %get-tuple-element.9), channel_id=1, replica_groups=mesh['level'=2,'gx'=4,'yz'=4] {'yz'}, use_global_device_ids=true, to_apply=%region_55.56 | all-reduce | flops 2 | bytes 16 | tf_op jit(solution)/shard_map/psum | solution.py:49
  534.9 11.0 %all-reduce.52 = (f32[]{:T(128)}, f32[]{:T(128)}) all-reduce(f32[]{:T(128)} %get-tuple-element.33, f32[]{:T(128)} %get-tuple-element.34), channel_id=1, replica_groups=mesh['level'=2,'gx'=4,'yz'=4] {'gx'}, use_global_device_ids=true, to_apply=%region_56.57 | all-reduce | flops 2 | bytes 16 | tf_op jit(solution)/shard_map/psum | solution.py:49
  565.1 11.3 %all-reduce.39 = (f32[]{:T(128)}, f32[]{:T(128)}) all-reduce(f32[]{:T(128)} %get-tuple-element.8, f32[]{:T(128)} %get-tuple-element.7), channel_id=1, replica_groups=mesh['level'=2,'gx'=4,'yz'=4] {'yz'}, use_global_device_ids=true, to_apply=%region_61.62 | all-reduce | flops 2 | bytes 16 | tf_op jit(solution)/shard_map/psum | solution.py:49
  576.4 11.0 %all-reduce.51 = (f32[]{:T(128)}, f32[]{:T(128)}) all-reduce(f32[]{:T(128)} %get-tuple-element.31, f32[]{:T(128)} %get-tuple-element.32), channel_id=1, replica_groups=mesh['level'=2,'gx'=4,'yz'=4] {'gx'}, use_global_device_ids=true, to_apply=%region_62.63 | all-reduce | flops 2 | bytes 16 | tf_op jit(solution)/shard_map/psum | solution.py:49
  610.0 11.3 %all-reduce.38 = (f32[]{:T(128)}, f32[]{:T(128)}) all-reduce(f32[]{:T(128)} %get-tuple-element.6, f32[]{:T(128)} %get-tuple-element.5), channel_id=1, replica_groups=mesh['level'=2,'gx'=4,'yz'=4] {'yz'}, use_global_device_ids=true, to_apply=%region_67.68 | all-reduce | flops 2 | bytes 16 | tf_op jit(solution)/shard_map/psum | solution.py:49
  621.3 11.0 %all-reduce.50 = (f32[]{:T(128)}, f32[]{:T(128)}) all-reduce(f32[]{:T(128)} %get-tuple-element.29, f32[]{:T(128)} %get-tuple-element.30), channel_id=1, replica_groups=mesh['level'=2,'gx'=4,'yz'=4] {'gx'}, use_global_device_ids=true, to_apply=%region_68.69 | all-reduce | flops 2 | bytes 16 | tf_op jit(solution)/shard_map/psum | solution.py:49
  (261 shorter events, 282.0 us)
Async XLA Ops:
  110.4 6.8 %collective-permute-start.12 = (f32[1,16,256]{2,1,0:T(8,128)S(1)}, f32[1,16,256]{2,1,0:T(8,128)S(1)}, u32[]{:S(2)}, u32[]{:S(2)}) collective-permute-start(f32[1,16,256]{2,1,0:T(8,128)S(1)} %get-tuple-element.186), channel_id=1, source_target_pairs={{4,0},{8,4},{12,8},{5,1},{9,5},{13,9},{6,2},{10,6},{14,10},{7,3},{... | collective-permute-start | bytes 49160 | tf_op jit(solution)/shard_map/ppermute | solution.py:21
  153.5 11.0 %collective-permute-start.22 = (f32[1,16,256]{2,1,0:T(8,128)S(1)}, f32[1,16,256]{2,1,0:T(8,128)S(1)}, u32[]{:S(2)}, u32[]{:S(2)}) collective-permute-start(f32[1,16,256]{2,1,0:T(8,128)S(1)} %get-tuple-element.181), channel_id=1, source_target_pairs={{0,4},{4,8},{8,12},{1,5},{5,9},{9,13},{2,6},{6,10},{10,14},{3,7},{... | collective-permute-start | bytes 49160 | tf_op jit(solution)/shard_map/ppermute | solution.py:19
  155.1 9.3 %collective-permute-start.21 = (f32[1,16,256]{2,1,0:T(8,128)S(1)}, f32[1,16,256]{2,1,0:T(8,128)S(1)}, u32[]{:S(2)}, u32[]{:S(2)}) collective-permute-start(f32[1,16,256]{2,1,0:T(8,128)S(1)} %get-tuple-element.182), channel_id=1, source_target_pairs={{4,0},{8,4},{12,8},{5,1},{9,5},{13,9},{6,2},{10,6},{14,10},{7,3},{... | collective-permute-start | bytes 49160 | tf_op jit(solution)/shard_map/ppermute | solution.py:21
  157.5 12.9 %collective-permute-start.18 = (f32[1,16,256]{2,1,0:T(8,128)S(1)}, f32[1,16,256]{2,1,0:T(8,128)S(1)}, u32[]{:S(2)}, u32[]{:S(2)}) collective-permute-start(f32[1,16,256]{2,1,0:T(8,128)S(1)} %get-tuple-element.179), channel_id=1, source_target_pairs={{0,4},{4,8},{8,12},{1,5},{5,9},{9,13},{2,6},{6,10},{10,14},{3,7},{... | collective-permute-start | bytes 49160 | tf_op jit(solution)/shard_map/ppermute | solution.py:19
  163.2 7.2 %collective-permute-start.17 = (f32[1,16,256]{2,1,0:T(8,128)S(1)}, f32[1,16,256]{2,1,0:T(8,128)S(1)}, u32[]{:S(2)}, u32[]{:S(2)}) collective-permute-start(f32[1,16,256]{2,1,0:T(8,128)S(1)} %get-tuple-element.180), channel_id=1, source_target_pairs={{4,0},{8,4},{12,8},{5,1},{9,5},{13,9},{6,2},{10,6},{14,10},{7,3},{... | collective-permute-start | bytes 49160 | tf_op jit(solution)/shard_map/ppermute | solution.py:21
  164.6 12.2 %collective-permute-start.23 = (f32[34,1,256]{2,1,0:T(1,128)S(1)}, f32[34,1,256]{2,1,0:T(1,128)S(1)}, u32[]{:S(2)}, u32[]{:S(2)}) collective-permute-start(f32[34,1,256]{2,1,0:T(1,128)S(1)} %get-tuple-element.113), channel_id=1, source_target_pairs={{1,0},{2,1},{3,2},{5,4},{6,5},{7,6},{9,8},{10,9},{11,10},{13,12},{... | collective-permute-start | bytes 104456 | tf_op jit(solution)/shard_map/ppermute | solution.py:21
  165.9 10.9 %collective-permute-start.24 = (f32[34,1,256]{2,1,0:T(1,128)S(1)}, f32[34,1,256]{2,1,0:T(1,128)S(1)}, u32[]{:S(2)}, u32[]{:S(2)}) collective-permute-start(f32[34,1,256]{2,1,0:T(1,128)S(1)} %get-tuple-element.114), channel_id=1, source_target_pairs={{0,1},{1,2},{2,3},{4,5},{5,6},{6,7},{8,9},{9,10},{10,11},{12,13},{... | collective-permute-start | bytes 104456 | tf_op jit(solution)/shard_map/ppermute | solution.py:19
  178.9 6.9 %collective-permute-start.26 = (f32[1,16,256]{2,1,0:T(8,128)S(1)}, f32[1,16,256]{2,1,0:T(8,128)S(1)}, u32[]{:S(2)}, u32[]{:S(2)}) collective-permute-start(f32[1,16,256]{2,1,0:T(8,128)S(1)} %get-tuple-element.171), channel_id=1, source_target_pairs={{0,4},{4,8},{8,12},{1,5},{5,9},{9,13},{2,6},{6,10},{10,14},{3,7},{... | collective-permute-start | bytes 49160 | tf_op jit(solution)/shard_map/ppermute | solution.py:19
  184.4 6.5 %collective-permute-start.25 = (f32[1,16,256]{2,1,0:T(8,128)S(1)}, f32[1,16,256]{2,1,0:T(8,128)S(1)}, u32[]{:S(2)}, u32[]{:S(2)}) collective-permute-start(f32[1,16,256]{2,1,0:T(8,128)S(1)} %get-tuple-element.172), channel_id=1, source_target_pairs={{4,0},{8,4},{12,8},{5,1},{9,5},{13,9},{6,2},{10,6},{14,10},{7,3},{... | collective-permute-start | bytes 49160 | tf_op jit(solution)/shard_map/ppermute | solution.py:21
  226.1 6.8 %collective-permute-start.29 = (f32[1,16,256]{2,1,0:T(8,128)S(1)}, f32[1,16,256]{2,1,0:T(8,128)S(1)}, u32[]{:S(2)}, u32[]{:S(2)}) collective-permute-start(f32[1,16,256]{2,1,0:T(8,128)S(1)} %get-tuple-element.168), channel_id=1, source_target_pairs={{4,0},{8,4},{12,8},{5,1},{9,5},{13,9},{6,2},{10,6},{14,10},{7,3},{... | collective-permute-start | bytes 49160 | tf_op jit(solution)/shard_map/ppermute | solution.py:21
  271.8 6.8 %collective-permute-start.33 = (f32[1,16,256]{2,1,0:T(8,128)S(1)}, f32[1,16,256]{2,1,0:T(8,128)S(1)}, u32[]{:S(2)}, u32[]{:S(2)}) collective-permute-start(f32[1,16,256]{2,1,0:T(8,128)S(1)} %get-tuple-element.166), channel_id=1, source_target_pairs={{4,0},{8,4},{12,8},{5,1},{9,5},{13,9},{6,2},{10,6},{14,10},{7,3},{... | collective-permute-start | bytes 49160 | tf_op jit(solution)/shard_map/ppermute | solution.py:21
  315.1 11.3 %collective-permute-start.43 = (f32[1,16,256]{2,1,0:T(8,128)S(1)}, f32[1,16,256]{2,1,0:T(8,128)S(1)}, u32[]{:S(2)}, u32[]{:S(2)}) collective-permute-start(f32[1,16,256]{2,1,0:T(8,128)S(1)} %get-tuple-element.161), channel_id=1, source_target_pairs={{0,4},{4,8},{8,12},{1,5},{5,9},{9,13},{2,6},{6,10},{10,14},{3,7},{... | collective-permute-start | bytes 49160 | tf_op jit(solution)/shard_map/ppermute | solution.py:19
  316.7 9.7 %collective-permute-start.42 = (f32[1,16,256]{2,1,0:T(8,128)S(1)}, f32[1,16,256]{2,1,0:T(8,128)S(1)}, u32[]{:S(2)}, u32[]{:S(2)}) collective-permute-start(f32[1,16,256]{2,1,0:T(8,128)S(1)} %get-tuple-element.162), channel_id=1, source_target_pairs={{4,0},{8,4},{12,8},{5,1},{9,5},{13,9},{6,2},{10,6},{14,10},{7,3},{... | collective-permute-start | bytes 49160 | tf_op jit(solution)/shard_map/ppermute | solution.py:21
  319.2 13.1 %collective-permute-start.39 = (f32[1,16,256]{2,1,0:T(8,128)S(1)}, f32[1,16,256]{2,1,0:T(8,128)S(1)}, u32[]{:S(2)}, u32[]{:S(2)}) collective-permute-start(f32[1,16,256]{2,1,0:T(8,128)S(1)} %get-tuple-element.159), channel_id=1, source_target_pairs={{0,4},{4,8},{8,12},{1,5},{5,9},{9,13},{2,6},{6,10},{10,14},{3,7},{... | collective-permute-start | bytes 49160 | tf_op jit(solution)/shard_map/ppermute | solution.py:19
  324.9 7.4 %collective-permute-start.38 = (f32[1,16,256]{2,1,0:T(8,128)S(1)}, f32[1,16,256]{2,1,0:T(8,128)S(1)}, u32[]{:S(2)}, u32[]{:S(2)}) collective-permute-start(f32[1,16,256]{2,1,0:T(8,128)S(1)} %get-tuple-element.160), channel_id=1, source_target_pairs={{4,0},{8,4},{12,8},{5,1},{9,5},{13,9},{6,2},{10,6},{14,10},{7,3},{... | collective-permute-start | bytes 49160 | tf_op jit(solution)/shard_map/ppermute | solution.py:21
  326.5 12.2 %collective-permute-start.44 = (f32[34,1,256]{2,1,0:T(1,128)S(1)}, f32[34,1,256]{2,1,0:T(1,128)S(1)}, u32[]{:S(2)}, u32[]{:S(2)}) collective-permute-start(f32[34,1,256]{2,1,0:T(1,128)S(1)} %get-tuple-element.103), channel_id=1, source_target_pairs={{1,0},{2,1},{3,2},{5,4},{6,5},{7,6},{9,8},{10,9},{11,10},{13,12},{... | collective-permute-start | bytes 104456 | tf_op jit(solution)/shard_map/ppermute | solution.py:21
  327.8 10.9 %collective-permute-start.45 = (f32[34,1,256]{2,1,0:T(1,128)S(1)}, f32[34,1,256]{2,1,0:T(1,128)S(1)}, u32[]{:S(2)}, u32[]{:S(2)}) collective-permute-start(f32[34,1,256]{2,1,0:T(1,128)S(1)} %get-tuple-element.104), channel_id=1, source_target_pairs={{0,1},{1,2},{2,3},{4,5},{5,6},{6,7},{8,9},{9,10},{10,11},{12,13},{... | collective-permute-start | bytes 104456 | tf_op jit(solution)/shard_map/ppermute | solution.py:19
  340.8 6.9 %collective-permute-start.47 = (f32[1,16,256]{2,1,0:T(8,128)S(1)}, f32[1,16,256]{2,1,0:T(8,128)S(1)}, u32[]{:S(2)}, u32[]{:S(2)}) collective-permute-start(f32[1,16,256]{2,1,0:T(8,128)S(1)} %get-tuple-element.151), channel_id=1, source_target_pairs={{0,4},{4,8},{8,12},{1,5},{5,9},{9,13},{2,6},{6,10},{10,14},{3,7},{... | collective-permute-start | bytes 49160 | tf_op jit(solution)/shard_map/ppermute | solution.py:19
  346.3 6.5 %collective-permute-start.46 = (f32[1,16,256]{2,1,0:T(8,128)S(1)}, f32[1,16,256]{2,1,0:T(8,128)S(1)}, u32[]{:S(2)}, u32[]{:S(2)}) collective-permute-start(f32[1,16,256]{2,1,0:T(8,128)S(1)} %get-tuple-element.152), channel_id=1, source_target_pairs={{4,0},{8,4},{12,8},{5,1},{9,5},{13,9},{6,2},{10,6},{14,10},{7,3},{... | collective-permute-start | bytes 49160 | tf_op jit(solution)/shard_map/ppermute | solution.py:21
  388.0 6.8 %collective-permute-start.50 = (f32[1,16,256]{2,1,0:T(8,128)S(1)}, f32[1,16,256]{2,1,0:T(8,128)S(1)}, u32[]{:S(2)}, u32[]{:S(2)}) collective-permute-start(f32[1,16,256]{2,1,0:T(8,128)S(1)} %get-tuple-element.148), channel_id=1, source_target_pairs={{4,0},{8,4},{12,8},{5,1},{9,5},{13,9},{6,2},{10,6},{14,10},{7,3},{... | collective-permute-start | bytes 49160 | tf_op jit(solution)/shard_map/ppermute | solution.py:21
  433.8 6.8 %collective-permute-start.54 = (f32[1,16,256]{2,1,0:T(8,128)S(1)}, f32[1,16,256]{2,1,0:T(8,128)S(1)}, u32[]{:S(2)}, u32[]{:S(2)}) collective-permute-start(f32[1,16,256]{2,1,0:T(8,128)S(1)} %get-tuple-element.146), channel_id=1, source_target_pairs={{4,0},{8,4},{12,8},{5,1},{9,5},{13,9},{6,2},{10,6},{14,10},{7,3},{... | collective-permute-start | bytes 49160 | tf_op jit(solution)/shard_map/ppermute | solution.py:21
  477.0 10.5 %collective-permute-start.64 = (f32[1,16,256]{2,1,0:T(8,128)S(1)}, f32[1,16,256]{2,1,0:T(8,128)S(1)}, u32[]{:S(2)}, u32[]{:S(2)}) collective-permute-start(f32[1,16,256]{2,1,0:T(8,128)S(1)} %get-tuple-element.141), channel_id=1, source_target_pairs={{0,4},{4,8},{8,12},{1,5},{5,9},{9,13},{2,6},{6,10},{10,14},{3,7},{... | collective-permute-start | bytes 49160 | tf_op jit(solution)/shard_map/ppermute | solution.py:19
  478.6 8.8 %collective-permute-start.63 = (f32[1,16,256]{2,1,0:T(8,128)S(1)}, f32[1,16,256]{2,1,0:T(8,128)S(1)}, u32[]{:S(2)}, u32[]{:S(2)}) collective-permute-start(f32[1,16,256]{2,1,0:T(8,128)S(1)} %get-tuple-element.142), channel_id=1, source_target_pairs={{4,0},{8,4},{12,8},{5,1},{9,5},{13,9},{6,2},{10,6},{14,10},{7,3},{... | collective-permute-start | bytes 49160 | tf_op jit(solution)/shard_map/ppermute | solution.py:21
  480.4 13.0 %collective-permute-start.60 = (f32[1,16,256]{2,1,0:T(8,128)S(1)}, f32[1,16,256]{2,1,0:T(8,128)S(1)}, u32[]{:S(2)}, u32[]{:S(2)}) collective-permute-start(f32[1,16,256]{2,1,0:T(8,128)S(1)} %get-tuple-element.139), channel_id=1, source_target_pairs={{0,4},{4,8},{8,12},{1,5},{5,9},{9,13},{2,6},{6,10},{10,14},{3,7},{... | collective-permute-start | bytes 49160 | tf_op jit(solution)/shard_map/ppermute | solution.py:19
  486.1 7.2 %collective-permute-start.59 = (f32[1,16,256]{2,1,0:T(8,128)S(1)}, f32[1,16,256]{2,1,0:T(8,128)S(1)}, u32[]{:S(2)}, u32[]{:S(2)}) collective-permute-start(f32[1,16,256]{2,1,0:T(8,128)S(1)} %get-tuple-element.140), channel_id=1, source_target_pairs={{4,0},{8,4},{12,8},{5,1},{9,5},{13,9},{6,2},{10,6},{14,10},{7,3},{... | collective-permute-start | bytes 49160 | tf_op jit(solution)/shard_map/ppermute | solution.py:21
  487.5 12.2 %collective-permute-start.65 = (f32[34,1,256]{2,1,0:T(1,128)S(1)}, f32[34,1,256]{2,1,0:T(1,128)S(1)}, u32[]{:S(2)}, u32[]{:S(2)}) collective-permute-start(f32[34,1,256]{2,1,0:T(1,128)S(1)} %get-tuple-element.93), channel_id=1, source_target_pairs={{1,0},{2,1},{3,2},{5,4},{6,5},{7,6},{9,8},{10,9},{11,10},{13,12},{... | collective-permute-start | bytes 104456 | tf_op jit(solution)/shard_map/ppermute | solution.py:21
  488.8 10.9 %collective-permute-start.66 = (f32[34,1,256]{2,1,0:T(1,128)S(1)}, f32[34,1,256]{2,1,0:T(1,128)S(1)}, u32[]{:S(2)}, u32[]{:S(2)}) collective-permute-start(f32[34,1,256]{2,1,0:T(1,128)S(1)} %get-tuple-element.94), channel_id=1, source_target_pairs={{0,1},{1,2},{2,3},{4,5},{5,6},{6,7},{8,9},{9,10},{10,11},{12,13},{... | collective-permute-start | bytes 104456 | tf_op jit(solution)/shard_map/ppermute | solution.py:19
  501.8 6.9 %collective-permute-start.68 = (f32[1,16,256]{2,1,0:T(8,128)S(1)}, f32[1,16,256]{2,1,0:T(8,128)S(1)}, u32[]{:S(2)}, u32[]{:S(2)}) collective-permute-start(f32[1,16,256]{2,1,0:T(8,128)S(1)} %get-tuple-element.131), channel_id=1, source_target_pairs={{0,4},{4,8},{8,12},{1,5},{5,9},{9,13},{2,6},{6,10},{10,14},{3,7},{... | collective-permute-start | bytes 49160 | tf_op jit(solution)/shard_map/ppermute | solution.py:19
  507.3 6.5 %collective-permute-start.67 = (f32[1,16,256]{2,1,0:T(8,128)S(1)}, f32[1,16,256]{2,1,0:T(8,128)S(1)}, u32[]{:S(2)}, u32[]{:S(2)}) collective-permute-start(f32[1,16,256]{2,1,0:T(8,128)S(1)} %get-tuple-element.132), channel_id=1, source_target_pairs={{4,0},{8,4},{12,8},{5,1},{9,5},{13,9},{6,2},{10,6},{14,10},{7,3},{... | collective-permute-start | bytes 49160 | tf_op jit(solution)/shard_map/ppermute | solution.py:21
  515.2 6.5 %collective-permute-start.70 = (f32[34,1,256]{2,1,0:T(1,128)S(1)}, f32[34,1,256]{2,1,0:T(1,128)S(1)}, u32[]{:S(2)}, u32[]{:S(2)}) collective-permute-start(f32[34,1,256]{2,1,0:T(1,128)S(1)} %get-tuple-element.90), channel_id=1, source_target_pairs={{0,1},{1,2},{2,3},{4,5},{5,6},{6,7},{8,9},{9,10},{10,11},{12,13},{... | collective-permute-start | bytes 104456 | tf_op jit(solution)/shard_map/ppermute | solution.py:19
  548.9 6.8 %collective-permute-start.71 = (f32[1,16,256]{2,1,0:T(8,128)S(1)}, f32[1,16,256]{2,1,0:T(8,128)S(1)}, u32[]{:S(2)}, u32[]{:S(2)}) collective-permute-start(f32[1,16,256]{2,1,0:T(8,128)S(1)} %get-tuple-element.128), channel_id=1, source_target_pairs={{4,0},{8,4},{12,8},{5,1},{9,5},{13,9},{6,2},{10,6},{14,10},{7,3},{... | collective-permute-start | bytes 49160 | tf_op jit(solution)/shard_map/ppermute | solution.py:21
  594.7 6.8 %collective-permute-start.75 = (f32[1,16,256]{2,1,0:T(8,128)S(1)}, f32[1,16,256]{2,1,0:T(8,128)S(1)}, u32[]{:S(2)}, u32[]{:S(2)}) collective-permute-start(f32[1,16,256]{2,1,0:T(8,128)S(1)} %get-tuple-element.126), channel_id=1, source_target_pairs={{4,0},{8,4},{12,8},{5,1},{9,5},{13,9},{6,2},{10,6},{14,10},{7,3},{... | collective-permute-start | bytes 49160 | tf_op jit(solution)/shard_map/ppermute | solution.py:21
  (57 other events, 308.0 us)
